TPU v7x, 32 devices: a whole 2x2x4 slice. The times are simulated.
32 devices in a mesh: ens: 4 (over y, x), lon: 8 (over z, core).
Axes of the slice: x: 2, y: 2, z: 4, core: 2. Of those that a mesh axis runs over, the one named last changes fastest.
Arguments:
- control: float32 [8, 1024, 512], P('ens', None, 'lon'), may hold values from -6 to 6
- residual: float32 [8, 1024, 512], P('ens', None, 'lon'), may hold values from -6 to 6
- direction: float32 [8, 1024, 512], P('ens', None, 'lon'), may hold values from -6 to 6
- ens_perturb: bfloat16 [8, 3, 1024, 512], P('ens', None, None, 'lon'), may hold values from -1.5 to 1.5
- localize: float32 [1024, 1024], replicated, may hold values from -0.5 to 1.5
- obs_cell: int32 [32768], P('lon'), may hold values from 0 to 65535
- obs_slot: int32 [32768], P('lon'), may hold values from 0 to 3
- obs_weight: float32 [32768], P('lon'), may hold values from 0.5 to 4
Outputs:
- control_new: float32 [8, 1024, 512], P('ens', None, 'lon')
- residual_new: float32 [8, 1024, 512], P('ens', None, 'lon')
- direction_new: float32 [8, 1024, 512], P('ens', None, 'lon')
Inputs may be any that keep to these rules, and one draw needn't show every extreme that they name: `obs_cell`: row-major cell within the entry's own longitude tile: row times 64 plus column. `obs_slot`: slot n < 3 observes the height after model step n + 1; slot 3 marks a padding entry that observes nothing.
All inputs are finite; a program needn't handle non-finite values.
Results may differ from a plain program's by a relative error of at most 0.0003.
Values sent between devices are 32-bit elements; how exact they have to be, the bound alone decides.
A program may use at most 64 MiB of HBM per device.

v0:
```python
import jax
import jax.numpy as jnp
from jax import lax
from jax.sharding import PartitionSpec as P

STEPS = 3
wave_speed = 0.35
rotation = 0.2


def extended(block, sides, width):
    for axis, dim in sides:
        count = lax.axis_size(axis)
        forward = [(i, i + 1) for i in range(count - 1)]
        forward.append((count - 1, 0))
        backward = [(target, source) for source, target in forward]
        low = lax.ppermute(
            lax.slice_in_dim(block, block.shape[dim] - width, None, axis=dim), axis, forward
        )
        high = lax.ppermute(lax.slice_in_dim(block, 0, width, axis=dim), axis, backward)
        block = jnp.concatenate([low, block, high], axis=dim)
    return block


def grid_factors(row_ids, lat_total):
    latitude = (-1.0 / 3.0 + 2.0 / 3.0 * (row_ids + 0.5) / lat_total) * jnp.pi
    return (1.0 / jnp.cos(latitude), jnp.sin(latitude))


def model_step(fields, orient, metric, coriolis):
    lon_wide = extended(fields, (("lon", 2),), 1)
    lat_wide = jnp.pad(fields, ((0, 0), (1, 1), (0, 0)))
    lon_diff = 0.5 * metric[:, None] * (lon_wide[:, :, 2:] - lon_wide[:, :, :-2])
    lat_diff = 0.5 * (lat_wide[:, 2:] - lat_wide[:, :-2])
    height, zonal, meridional = (fields[0], fields[1], fields[2])
    speed = orient * wave_speed
    turning = orient * rotation * coriolis[:, None]
    return jnp.stack(
        [
            height - speed * (lon_diff[1] + lat_diff[2]),
            zonal - speed * lon_diff[0] + turning * meridional,
            meridional - speed * lat_diff[0] - turning * zonal,
        ]
    )


def body(control, residual, direction, ens_perturb, localize, obs_cell, obs_slot, obs_weight):
    hi = lax.Precision.HIGHEST
    lat_total = localize.shape[0]
    tile_cols = control.shape[2]
    localized = jnp.einsum("ij,mjc->mic", localize, direction, precision=hi)
    increment = jnp.sum(ens_perturb.astype(jnp.float32) * localized[:, None], axis=0)
    lat_slab = lax.psum(increment, "ens")
    slab_rows = lat_slab.shape[1]
    cells = slab_rows * tile_cols
    row_ids = jnp.arange(slab_rows, dtype=jnp.int32).astype(jnp.float32)
    metric, coriolis = grid_factors(row_ids, lat_total)
    local_row = obs_cell // tile_cols
    inside = (local_row >= 0) & (local_row < slab_rows) & (obs_slot < STEPS)
    cell_index = jnp.clip(local_row, 0, slab_rows - 1) * tile_cols + obs_cell % tile_cols
    slot_index = obs_slot * cells + cell_index
    gather_index = jnp.clip(slot_index, 0, STEPS * cells - 1)
    tl_state = lat_slab
    heights = []
    for moment in range(STEPS):
        tl_state = model_step(tl_state, 1.0, metric, coriolis)
        heights.append(tl_state[0].reshape(-1))
    observed = jnp.concatenate(heights)[gather_index]
    weighted = jnp.where(inside, obs_weight * observed, 0.0)
    forcing = jnp.zeros(((STEPS + 1) * cells,), jnp.float32).at[slot_index].add(weighted)
    forcing = forcing.reshape(STEPS + 1, slab_rows, tile_cols)
    adjoint = jnp.zeros(lat_slab.shape, jnp.float32)
    for moment in reversed(range(STEPS)):
        adjoint = adjoint.at[0].add(forcing[moment])
        adjoint = model_step(adjoint, -1.0, metric, coriolis)
    projected = jnp.sum(ens_perturb.astype(jnp.float32) * adjoint[None], axis=1)
    pulled_back = jnp.einsum("ji,mjc->mic", localize, projected, precision=hi)
    image_vec = direction + pulled_back
    norm_old, curvature, cross_term, square = lax.psum(
        (
            jnp.sum(residual * residual),
            jnp.sum(direction * image_vec),
            jnp.sum(residual * image_vec),
            jnp.sum(image_vec * image_vec),
        ),
        ("ens", "lon"),
    )
    step_size = norm_old / curvature
    control_new = control + step_size * direction
    residual_new = residual - step_size * image_vec
    norm_new = norm_old - 2.0 * step_size * cross_term + step_size * step_size * square
    direction_new = residual_new + norm_new / norm_old * direction
    return (control_new, residual_new, direction_new)


def solution(mesh):
    in_specs = (
        P("ens", None, "lon"),
        P("ens", None, "lon"),
        P("ens", None, "lon"),
        P("ens", None, None, "lon"),
        P(),
        P("lon"),
        P("lon"),
        P("lon"),
    )
    out_specs = (P("ens", None, "lon"), P("ens", None, "lon"), P("ens", None, "lon"))
    return jax.shard_map(body, mesh=mesh, in_specs=in_specs, out_specs=out_specs, check_vma=False)
```

profile of v0, /device:TPU:12, one launch (start us, length us, event | category | flops | bytes accessed | tf_op | source)
XLA Modules:
  0.0 210.3 jit_solution(16358781422589472048)
XLA Ops:
  7.2 6.8 %fusion.6 = f32[2,1024,64]{1,2,0:T(8,128)S(1)} fusion(f32[2,1024,64]{1,2,0:T(8,128)} %param.16, f32[1024,1024]{1,0:T(8,128)} %param.18), kind=kOutput, calls=%fused_computation.10 | convolution fusion | flops 1610612736 | bytes 5242880 | tf_op jit(solution)/shard_map/ij,mjc->mic/dot_general | solution.py:51
  14.1 1.1 fusion.4
  15.3 49.7 %all-reduce.10.cloned.1.call-done = f32[3,1024,64]{1,2,0:T(8,128)} async-done(((f32[3,1024,64]{1,2,0:T(8,128)}), f32[3,1024,64]{1,2,0:T(8,128)}) %all-reduce.10.cloned.1.call-update) | async-done | bytes 786448 | tf_op jit(solution)/shard_map/psum | solution.py:53
  65.0 1.0 fusion.89
  66.1 0.5 collective-permute-start.1
  66.6 0.9 collective-permute-done
  67.5 1.8 collective-permute-done.1
  69.2 2.8 %fusion.34 = (f32[3,1024,64]{1,2,0:T(8,128)S(1)}, f32[3,1024,64]{1,2,0:T(8,128)S(1)}) fusion(f32[3,1024,64]{1,2,0:T(8,128)} %all-reduce.10.cloned.1.call-done, f32[3,1024,1]{1,2,0:T(1,128)S(1)} %collective-permute-done.1, f32[3,1024,1]{1,2,0:T(1,128)S(1)} %collective-permute-done, f32[1024]{0:T(1024)S(1)} %divide_multiply_fusion), kind=kLoop, calls=%fused_computation.57 | loop fusion | flops 1179648 | bytes 2387968 | tf_op jit(solution)/shard_map/mul | solution.py:33
  72.0 1.3 fusion.70
  73.4 0.8 collective-permute-start.2
  74.2 0.5 fusion.18
  74.7 0.2 copy.12
  75.1 0.6 collective-permute-done.2
  75.6 4.2 %collective-permute-done.3 = f32[3,1024,1]{1,2,0:T(1,128)S(1)} collective-permute-done((f32[3,1024,1]{1,2,0:T(1,128)S(1)}, f32[3,1024,1]{1,2,0:T(1,128)S(1)}, u32[]{:S(2)}, u32[]{:S(2)}) %collective-permute-start.3) | collective-permute-done | bytes 12320 | tf_op jit(solution)/shard_map/ppermute | solution.py:17
  79.9 0.2 fusion.32
  80.0 0.9 fusion.82
  81.1 0.5 collective-permute-start.5
  81.6 1.3 pad_slice_fusion.7
  82.9 1.1 copy.13
  84.2 1.8 collective-permute-done.5
  86.1 1.1 fusion.57
  87.1 0.2 copy.14
  87.6 23.0 %gather_fusion = f32[4096]{0:T(1024)S(1)} fusion(f32[196608]{0:T(1024)S(1)} %pad_maximum_fusion.16, s32[4096]{0:T(1024)S(1)} %get-tuple-element.53), kind=kCustom, calls=%fused_computation | custom fusion | bytes 49152 | tf_op jit(solution)/shard_map/gather | solution.py:68
  110.7 22.2 %scatter_custom_fusion = f32[262144]{0:T(1024)S(1)} fusion(s32[4096]{0:T(1024)S(1)} %compare_select_fusion.1, f32[4096]{0:T(1024)S(1)} %multiply_select_fusion, f32[]{:T(128)} %constant.120.clone.1), kind=kCustom, calls=%fused_computation.71 | custom fusion | flops 4096 | bytes 1048580 | tf_op jit(solution)/shard_map/scatter-add | solution.py:70
  132.9 0.1 slice.347
  133.1 0.2 copy.16
  133.3 1.3 collective-permute-start.6
  134.7 0.1 slice.357
  134.9 0.2 copy.17
  135.1 0.9 collective-permute-done.6
  136.0 2.3 %collective-permute-done.7 = f32[3,1024,1]{1,2,0:T(1,128)S(1)} collective-permute-done((f32[3,1024,1]{1,2,0:T(1,128)S(1)}, f32[3,1024,1]{1,2,0:T(1,128)S(1)}, u32[]{:S(2)}, u32[]{:S(2)}) %collective-permute-start.7) | collective-permute-done | bytes 12320 | tf_op jit(solution)/shard_map/ppermute | solution.py:17
  138.3 0.6 fusion.30
  139.2 0.6 collective-permute-start.8
  139.8 0.2 slice.370
  140.0 0.2 copy.18
  140.2 1.0 collective-permute-done.8
  141.2 4.2 %collective-permute-done.9 = f32[3,1024,1]{1,2,0:T(1,128)S(1)} collective-permute-done((f32[3,1024,1]{1,2,0:T(1,128)S(1)}, f32[3,1024,1]{1,2,0:T(1,128)S(1)}, u32[]{:S(2)}, u32[]{:S(2)}) %collective-permute-start.9) | collective-permute-done | bytes 12320 | tf_op jit(solution)/shard_map/ppermute | solution.py:17
  145.4 0.6 fusion.28
  146.0 0.2 fusion.46
  146.4 0.5 collective-permute-start.11
  146.9 0.9 collective-permute-done.10
  147.8 3.8 %collective-permute-done.11 = f32[3,1024,1]{1,2,0:T(1,128)S(1)} collective-permute-done((f32[3,1024,1]{1,2,0:T(1,128)S(1)}, f32[3,1024,1]{1,2,0:T(1,128)S(1)}, u32[]{:S(2)}, u32[]{:S(2)}) %collective-permute-start.11) | collective-permute-done | bytes 12320 | tf_op jit(solution)/shard_map/ppermute | solution.py:17
  151.5 0.6 fusion.26
  152.1 0.2 fusion.40
  152.4 0.2 fusion.5
  152.6 3.1 %multiply_reduce_fusion = (f32[]{:T(128)}, f32[]{:T(128)}, f32[]{:T(128)}, f32[]{:T(128)}, f32[2,1024,64]{1,2,0:T(8,128)S(1)}) fusion(f32[2,1024,64]{1,2,0:T(8,128)S(1)} %copy-done.3, f32[2,1024,64]{1,2,0:T(8,128)S(1)} %copy-done.1, f32[2,1024,64]{1,2,0:T(8,128)S(1)} %fusion.5, f32[1024,1024]{1,0:T(8,128)S(1)} %copy-done), kind=kOutput, calls=%fused_computation.66 | convolution fusion | flops 1611792384 | bytes 6291472 | tf_op jit(solution)/shard_map/ji,mjc->mic/dot_general | solution.py:77
  155.7 42.6 %all-reduce.7 = (f32[]{:T(128)}, f32[]{:T(128)}, f32[]{:T(128)}, f32[]{:T(128)}) all-reduce(f32[]{:T(128)} %get-tuple-element.41, f32[]{:T(128)} %get-tuple-element.42, f32[]{:T(128)} %get-tuple-element.40, f32[]{:T(128)} %get-tuple-element.39), channel_id=1, replica_groups=mesh['ens'=4,'lon'=8] {'ens','lon'}, use_global_device_ids=true, to_apply=%region_1.0 | all-reduce | flops 4 | bytes 32 | tf_op jit(solution)/shard_map/psum | solution.py:79
  202.2 1.3 multiply_add_fusion
  (52 shorter events, 1.8 us)
Async XLA Ops:
  7.2 6.9 %copy-start.2 = (bf16[2,3,1024,64]{2,3,1,0:T(8,128)(2,1)S(1)}, bf16[2,3,1024,64]{2,3,1,0:T(8,128)(2,1)}, u32[]{:S(2)}) copy-start(bf16[2,3,1024,64]{2,3,1,0:T(8,128)(2,1)} %param.17) | copy-start | bytes 2359300
  7.2 8.1 %copy-start.5 = (s32[4096]{0:T(1024)S(1)}, s32[4096]{0:T(1024)}, u32[]{:S(2)}) copy-start(s32[4096]{0:T(1024)} %param.19) | copy-start | bytes 49156
  7.2 8.1 %copy-start.6 = (s32[4096]{0:T(1024)S(1)}, s32[4096]{0:T(1024)}, u32[]{:S(2)}) copy-start(s32[4096]{0:T(1024)} %param.20) | copy-start | bytes 49156
  7.2 57.8 %all-reduce.10.cloned.1.call-start = ((), (), s32[]{:S(2)}) async-start(), calls=%async_computation | async-start | bytes 1572864 | tf_op jit(solution)/shard_map/psum | solution.py:53
  66.0 1.5 collective-permute-start
  66.1 3.2 %collective-permute-start.1 = (f32[3,1024,1]{1,2,0:T(1,128)S(1)}, f32[3,1024,1]{1,2,0:T(1,128)S(1)}, u32[]{:S(2)}, u32[]{:S(2)}) collective-permute-start(f32[3,1024,1]{1,2,0:T(1,128)S(1)} %get-tuple-element.95), channel_id=1, source_target_pairs={{0,1},{1,2},{2,3},{3,4},{4,5},{5,6},{6,7},{7,0},{8,9},{9,10},{10,1... | collective-permute-start | bytes 36872 | tf_op jit(solution)/shard_map/ppermute | solution.py:17
  73.4 2.2 %collective-permute-start.2 = (f32[3,1024,1]{1,2,0:T(1,128)S(1)}, f32[3,1024,1]{1,2,0:T(1,128)S(1)}, u32[]{:S(2)}, u32[]{:S(2)}) collective-permute-start(f32[3,1024,1]{1,2,0:T(1,128)S(1)} %get-tuple-element.90), channel_id=1, source_target_pairs={{1,0},{2,1},{3,2},{4,3},{5,4},{6,5},{7,6},{0,7},{9,8},{10,9},{11,1... | collective-permute-start | bytes 36872 | tf_op jit(solution)/shard_map/ppermute | solution.py:20
  74.2 5.6 %collective-permute-start.3 = (f32[3,1024,1]{1,2,0:T(1,128)S(1)}, f32[3,1024,1]{1,2,0:T(1,128)S(1)}, u32[]{:S(2)}, u32[]{:S(2)}) collective-permute-start(f32[3,1024,1]{1,2,0:T(1,128)S(1)} %get-tuple-element.91), channel_id=1, source_target_pairs={{0,1},{1,2},{2,3},{3,4},{4,5},{5,6},{6,7},{7,0},{8,9},{9,10},{10,1... | collective-permute-start | bytes 36872 | tf_op jit(solution)/shard_map/ppermute | solution.py:17
  81.0 3.2 %collective-permute-start.4 = (f32[3,1024,1]{1,2,0:T(1,128)S(1)}, f32[3,1024,1]{1,2,0:T(1,128)S(1)}, u32[]{:S(2)}, u32[]{:S(2)}) collective-permute-start(f32[3,1024,1]{1,2,0:T(1,128)S(1)} %get-tuple-element.85), channel_id=1, source_target_pairs={{1,0},{2,1},{3,2},{4,3},{5,4},{6,5},{7,6},{0,7},{9,8},{10,9},{11,1... | collective-permute-start | bytes 36872 | tf_op jit(solution)/shard_map/ppermute | solution.py:20
  81.1 5.0 %collective-permute-start.5 = (f32[3,1024,1]{1,2,0:T(1,128)S(1)}, f32[3,1024,1]{1,2,0:T(1,128)S(1)}, u32[]{:S(2)}, u32[]{:S(2)}) collective-permute-start(f32[3,1024,1]{1,2,0:T(1,128)S(1)} %get-tuple-element.84), channel_id=1, source_target_pairs={{0,1},{1,2},{2,3},{3,4},{4,5},{5,6},{6,7},{7,0},{8,9},{9,10},{10,1... | collective-permute-start | bytes 36872 | tf_op jit(solution)/shard_map/ppermute | solution.py:17
  87.6 23.1 %copy-start.7 = (f32[4096]{0:T(1024)S(1)}, f32[4096]{0:T(1024)}, u32[]{:S(2)}) copy-start(f32[4096]{0:T(1024)} %param.21) | copy-start | bytes 49156
  133.3 2.7 %collective-permute-start.6 = (f32[3,1024,1]{1,2,0:T(1,128)S(1)}, f32[3,1024,1]{1,2,0:T(1,128)S(1)}, u32[]{:S(2)}, u32[]{:S(2)}) collective-permute-start(f32[3,1024,1]{1,2,0:T(1,128)S(1)} %get-tuple-element.97), channel_id=1, source_target_pairs={{1,0},{2,1},{3,2},{4,3},{5,4},{6,5},{7,6},{0,7},{9,8},{10,9},{11,1... | collective-permute-start | bytes 36872 | tf_op jit(solution)/shard_map/ppermute | solution.py:20
  134.6 3.7 %collective-permute-start.7 = (f32[3,1024,1]{1,2,0:T(1,128)S(1)}, f32[3,1024,1]{1,2,0:T(1,128)S(1)}, u32[]{:S(2)}, u32[]{:S(2)}) collective-permute-start(f32[3,1024,1]{1,2,0:T(1,128)S(1)} %get-tuple-element.98), channel_id=1, source_target_pairs={{0,1},{1,2},{2,3},{3,4},{4,5},{5,6},{6,7},{7,0},{8,9},{9,10},{10,1... | collective-permute-start | bytes 36872 | tf_op jit(solution)/shard_map/ppermute | solution.py:17
  139.2 2.0 collective-permute-start.8
  139.8 5.6 %collective-permute-start.9 = (f32[3,1024,1]{1,2,0:T(1,128)S(1)}, f32[3,1024,1]{1,2,0:T(1,128)S(1)}, u32[]{:S(2)}, u32[]{:S(2)}) collective-permute-start(f32[3,1024,1]{1,2,0:T(1,128)S(1)} %get-tuple-element.78), channel_id=1, source_target_pairs={{0,1},{1,2},{2,3},{3,4},{4,5},{5,6},{6,7},{7,0},{8,9},{9,10},{10,1... | collective-permute-start | bytes 36872 | tf_op jit(solution)/shard_map/ppermute | solution.py:17
  146.3 1.5 collective-permute-start.10
  146.4 6.2 %copy-start = (f32[1024,1024]{1,0:T(8,128)S(1)}, f32[1024,1024]{1,0:T(8,128)}, u32[]{:S(2)}) copy-start(f32[1024,1024]{1,0:T(8,128)} %param.18) | copy-start | bytes 12582916
  146.4 6.2 %copy-start.1 = (f32[2,1024,64]{1,2,0:T(8,128)S(1)}, f32[2,1024,64]{1,2,0:T(8,128)}, u32[]{:S(2)}) copy-start(f32[2,1024,64]{1,2,0:T(8,128)} %param.16) | copy-start | bytes 1572868
  146.4 6.2 %copy-start.3 = (f32[2,1024,64]{1,2,0:T(8,128)S(1)}, f32[2,1024,64]{1,2,0:T(8,128)}, u32[]{:S(2)}) copy-start(f32[2,1024,64]{1,2,0:T(8,128)} %param.15) | copy-start | bytes 1572868
  146.4 5.1 %collective-permute-start.11 = (f32[3,1024,1]{1,2,0:T(1,128)S(1)}, f32[3,1024,1]{1,2,0:T(1,128)S(1)}, u32[]{:S(2)}, u32[]{:S(2)}) collective-permute-start(f32[3,1024,1]{1,2,0:T(1,128)S(1)} %get-tuple-element.74), channel_id=1, source_target_pairs={{0,1},{1,2},{2,3},{3,4},{4,5},{5,6},{6,7},{7,0},{8,9},{9,10},{10,1... | collective-permute-start | bytes 36872 | tf_op jit(solution)/shard_map/ppermute | solution.py:17
  152.3 49.9 %copy-start.4 = (f32[2,1024,64]{1,2,0:T(8,128)S(1)}, f32[2,1024,64]{1,2,0:T(8,128)}, u32[]{:S(2)}) copy-start(f32[2,1024,64]{1,2,0:T(8,128)} %param.14) | copy-start | bytes 1572868
Sparse Core Ops, SparseCore 0:
  15.3 49.6 all-reduce.9
where the time goes:
time: 211 us; the launch traced here: 210 us
  waiting for transfers between devices  72.1 us (34%)
  blocking collectives  42.6 us (20%)
  other arithmetic  34.3 us (16%)
  local copies, waits for them, and re-layouts  28.5 us (14%)
  between operations  18.5 us (9%)
  matrix products  9.88 us (5%)
  starting transfers between devices  4.47 us (2%)
    psum x1, waiting for transfers between devices, body(): lat_slab = lax.psum(increment, 'ens')  49.7 us
    psum x1, blocking collectives, body(): lax.psum((jnp.sum(residual * residual), jnp.sum(direction * image_vec), j...  42.6 us
    gather x1, local copies, waits for them, and re-layouts, body(): observed = jnp.concatenate(heights)[gather_index]  23 us
    scatter-add x1, other arithmetic, body(): jnp.zeros(((STEPS + 1) * cells,), jnp.float32).at[slot_index].add(weighted)  22.2 us
    ppermute x6, waiting for transfers between devices, extended(): lax.ppermute(lax.slice_in_dim(block, block.shape[dim] - width, None, axis...  18.1 us
    dot_general x1, matrix products, body(): localized = jnp.einsum('ij,mjc->mic', localize, direction, precision=hi)  6.79 us
    mul x6, other arithmetic, model_step(): 0.5 * metric[:, None] * (lon_wide[:, :, 2:] - lon_wide[:, :, :-2])  4.76 us
    ppermute x6, waiting for transfers between devices, extended(): lax.ppermute(lax.slice_in_dim(block, 0, width, axis=dim), axis, backward)  4.27 us
  transfers between devices with their start and end apart: 13, of which 12 were waited for; matrix products, arithmetic and copies ran while one was open for 2% of the time, Pallas kernels for 0%

commit v1 on v0

--- a/solution.py
+++ b/solution.py
@@ -50,7 +50,7 @@
     tile_cols = control.shape[2]
     localized = jnp.einsum("ij,mjc->mic", localize, direction, precision=hi)
     increment = jnp.sum(ens_perturb.astype(jnp.float32) * localized[:, None], axis=0)
-    lat_slab = lax.psum(increment, "ens")
+    lat_slab = lax.all_gather(increment, "ens").sum(axis=0)
     slab_rows = lat_slab.shape[1]
     cells = slab_rows * tile_cols
     row_ids = jnp.arange(slab_rows, dtype=jnp.int32).astype(jnp.float32)

time: 211 us -> 204 us (0.967)
  waiting for transfers between devices: 72.1 us -> 67.4 us
    psum x1 -> x0, waiting for transfers between devices: 49.7 us -> none  [body(): lat_slab = lax.psum(increment, 'ens')]
    all_gather x0 -> x1, waiting for transfers between devices: none -> 45 us  [body(): lat_slab = lax.all_gather(increment, 'ens').sum(axis=0)]
    reduce_sum x0 -> x1, other arithmetic: none -> 2.26 us  [body(): lat_slab = lax.all_gather(increment, 'ens').sum(axis=0)]
    mul x6, other arithmetic: 4.76 us -> 2.55 us  [model_step(): 0.5 * metric[:, None] * (lon_wide[:, :, 2:] - lon_wide[:, :, :-2])]
where the time goes in v1:
time: 204 us; the launch traced here: 203 us
  waiting for transfers between devices  67.4 us (33%)
  blocking collectives  42.5 us (21%)
  other arithmetic  33.2 us (16%)
  local copies, waits for them, and re-layouts  27.6 us (14%)
  between operations  18.5 us (9%)
  matrix products  9.88 us (5%)
  starting transfers between devices  4.44 us (2%)
    all_gather x1, waiting for transfers between devices, body(): lat_slab = lax.all_gather(increment, 'ens').sum(axis=0)  45 us
    psum x1, blocking collectives, body(): lax.psum((jnp.sum(residual * residual), jnp.sum(direction * image_vec), j...  42.5 us
    gather x1, local copies, waits for them, and re-layouts, body(): observed = jnp.concatenate(heights)[gather_index]  23 us
    scatter-add x1, other arithmetic, body(): jnp.zeros(((STEPS + 1) * cells,), jnp.float32).at[slot_index].add(weighted)  22.2 us
    ppermute x6, waiting for transfers between devices, extended(): lax.ppermute(lax.slice_in_dim(block, block.shape[dim] - width, None, axis...  18.1 us
    dot_general x1, matrix products, body(): localized = jnp.einsum('ij,mjc->mic', localize, direction, precision=hi)  6.79 us
    ppermute x6, waiting for transfers between devices, extended(): lax.ppermute(lax.slice_in_dim(block, 0, width, axis=dim), axis, backward)  4.27 us
  transfers between devices with their start and end apart: 13, of which 12 were waited for; matrix products, arithmetic and copies ran while one was open for 2% of the time, Pallas kernels for 0%

profile of v1, /device:TPU:12, one launch (start us, length us, event | category | flops | bytes accessed | tf_op | source)
XLA Modules:
  0.0 203.5 jit_solution(6216985833287400118)
XLA Ops:
  7.2 6.8 %fusion.6 = f32[2,1024,64]{1,2,0:T(8,128)S(1)} fusion(f32[2,1024,64]{1,2,0:T(8,128)} %param.16, f32[1024,1024]{1,0:T(8,128)} %param.18), kind=kOutput, calls=%fused_computation.10 | convolution fusion | flops 1610612736 | bytes 5242880 | tf_op jit(solution)/shard_map/ij,mjc->mic/dot_general | solution.py:51
  14.1 1.1 fusion.4
  15.3 45.0 %all-gather.3.cloned.1.call-done = f32[12,1024,64]{1,2,0:T(8,128)} async-done(((f32[3,1024,64]{1,2,0:T(8,128)}), f32[12,1024,64]{1,2,0:T(8,128)}) %all-gather.3.cloned.1.call-update) | async-done | bytes 3145744 | tf_op jit(solution)/shard_map/all_gather | solution.py:53
  60.3 2.3 %reduce_sum.65 = f32[3,1024,64]{1,2,0:T(8,128)S(1)} reduce(f32[4,3,1024,64]{2,3,1,0:T(8,128)} %bitcast.22, f32[]{:T(128)} %constant.120.clone.1), dimensions={0}, to_apply=%region_3.4 | reduce | flops 589824 | bytes 3932164 | tf_op jit(solution)/shard_map/reduce_sum | solution.py:53
  62.6 0.5 collective-permute-start.1
  63.2 0.9 collective-permute-done
  64.0 1.8 collective-permute-done.1
  65.8 0.6 fusion.34
  66.4 0.2 fusion.70
  66.7 0.8 collective-permute-start.2
  67.5 0.5 fusion.18
  67.9 0.2 copy.37
  68.3 0.6 collective-permute-done.2
  68.9 4.2 %collective-permute-done.3 = f32[3,1024,1]{1,2,0:T(1,128)S(1)} collective-permute-done((f32[3,1024,1]{1,2,0:T(1,128)S(1)}, f32[3,1024,1]{1,2,0:T(1,128)S(1)}, u32[]{:S(2)}, u32[]{:S(2)}) %collective-permute-start.3) | collective-permute-done | bytes 12320 | tf_op jit(solution)/shard_map/ppermute | solution.py:17
  73.1 0.2 fusion.32
  73.3 0.9 fusion.82
  74.3 0.5 collective-permute-start.5
  74.8 1.3 pad_slice_fusion.7
  76.2 1.1 copy.38
  77.5 1.8 collective-permute-done.5
  79.3 1.1 fusion.57
  80.4 0.2 copy.39
  80.8 23.0 %gather_fusion = f32[4096]{0:T(1024)S(1)} fusion(f32[196608]{0:T(1024)S(1)} %pad_maximum_fusion.16, s32[4096]{0:T(1024)S(1)} %get-tuple-element.53), kind=kCustom, calls=%fused_computation | custom fusion | bytes 49152 | tf_op jit(solution)/shard_map/gather | solution.py:68
  103.9 22.2 %scatter_custom_fusion = f32[262144]{0:T(1024)S(1)} fusion(s32[4096]{0:T(1024)S(1)} %compare_select_fusion.1, f32[4096]{0:T(1024)S(1)} %multiply_select_fusion, f32[]{:T(128)} %constant.120.clone.1), kind=kCustom, calls=%fused_computation.71 | custom fusion | flops 4096 | bytes 1048580 | tf_op jit(solution)/shard_map/scatter-add | solution.py:70
  126.1 0.1 slice.347
  126.3 0.2 copy.41
  126.5 1.3 collective-permute-start.6
  128.0 0.1 slice.357
  128.1 0.2 copy.42
  128.3 0.9 collective-permute-done.6
  129.2 2.3 %collective-permute-done.7 = f32[3,1024,1]{1,2,0:T(1,128)S(1)} collective-permute-done((f32[3,1024,1]{1,2,0:T(1,128)S(1)}, f32[3,1024,1]{1,2,0:T(1,128)S(1)}, u32[]{:S(2)}, u32[]{:S(2)}) %collective-permute-start.7) | collective-permute-done | bytes 12320 | tf_op jit(solution)/shard_map/ppermute | solution.py:17
  131.5 0.6 fusion.30
  132.4 0.6 collective-permute-start.8
  133.1 0.2 slice.370
  133.2 0.2 copy.43
  133.4 1.0 collective-permute-done.8
  134.4 4.2 %collective-permute-done.9 = f32[3,1024,1]{1,2,0:T(1,128)S(1)} collective-permute-done((f32[3,1024,1]{1,2,0:T(1,128)S(1)}, f32[3,1024,1]{1,2,0:T(1,128)S(1)}, u32[]{:S(2)}, u32[]{:S(2)}) %collective-permute-start.9) | collective-permute-done | bytes 12320 | tf_op jit(solution)/shard_map/ppermute | solution.py:17
  138.6 0.6 fusion.28
  139.2 0.2 fusion.46
  139.6 0.5 collective-permute-start.11
  140.1 0.9 collective-permute-done.10
  141.0 3.8 %collective-permute-done.11 = f32[3,1024,1]{1,2,0:T(1,128)S(1)} collective-permute-done((f32[3,1024,1]{1,2,0:T(1,128)S(1)}, f32[3,1024,1]{1,2,0:T(1,128)S(1)}, u32[]{:S(2)}, u32[]{:S(2)}) %collective-permute-start.11) | collective-permute-done | bytes 12320 | tf_op jit(solution)/shard_map/ppermute | solution.py:17
  144.8 0.6 fusion.26
  145.3 0.2 fusion.40
  145.6 0.2 fusion.5
  145.8 3.1 %multiply_reduce_fusion = (f32[]{:T(128)}, f32[]{:T(128)}, f32[]{:T(128)}, f32[]{:T(128)}, f32[2,1024,64]{1,2,0:T(8,128)S(1)}) fusion(f32[2,1024,64]{1,2,0:T(8,128)S(1)} %copy-done.3, f32[2,1024,64]{1,2,0:T(8,128)S(1)} %copy-done.1, f32[2,1024,64]{1,2,0:T(8,128)S(1)} %fusion.5, f32[1024,1024]{1,0:T(8,128)S(1)} %copy-done), kind=kOutput, calls=%fused_computation.66 | convolution fusion | flops 1611792384 | bytes 6291472 | tf_op jit(solution)/shard_map/ji,mjc->mic/dot_general | solution.py:77
  148.9 42.5 %all-reduce.7 = (f32[]{:T(128)}, f32[]{:T(128)}, f32[]{:T(128)}, f32[]{:T(128)}) all-reduce(f32[]{:T(128)} %get-tuple-element.41, f32[]{:T(128)} %get-tuple-element.42, f32[]{:T(128)} %get-tuple-element.40, f32[]{:T(128)} %get-tuple-element.39), channel_id=1, replica_groups=mesh['ens'=4,'lon'=8] {'ens','lon'}, use_global_device_ids=true, to_apply=%region_1.0 | all-reduce | flops 4 | bytes 32 | tf_op jit(solution)/shard_map/psum | solution.py:79
  195.4 1.3 multiply_add_fusion
  (53 shorter events, 1.8 us)
Async XLA Ops:
  7.2 6.9 %copy-start.2 = (bf16[2,3,1024,64]{2,3,1,0:T(8,128)(2,1)S(1)}, bf16[2,3,1024,64]{2,3,1,0:T(8,128)(2,1)}, u32[]{:S(2)}) copy-start(bf16[2,3,1024,64]{2,3,1,0:T(8,128)(2,1)} %param.17) | copy-start | bytes 2359300
  7.2 8.1 %copy-start.5 = (s32[4096]{0:T(1024)S(1)}, s32[4096]{0:T(1024)}, u32[]{:S(2)}) copy-start(s32[4096]{0:T(1024)} %param.19) | copy-start | bytes 49156
  7.2 8.1 %copy-start.6 = (s32[4096]{0:T(1024)S(1)}, s32[4096]{0:T(1024)}, u32[]{:S(2)}) copy-start(s32[4096]{0:T(1024)} %param.20) | copy-start | bytes 49156
  7.2 53.1 %all-gather.3.cloned.1.call-start = ((), (), s32[]{:S(2)}) async-start(), calls=%async_computation | async-start | bytes 3932160 | tf_op jit(solution)/shard_map/all_gather | solution.py:53
  62.6 1.5 collective-permute-start
  62.6 3.2 %collective-permute-start.1 = (f32[3,1024,1]{1,2,0:T(1,128)S(1)}, f32[3,1024,1]{1,2,0:T(1,128)S(1)}, u32[]{:S(2)}, u32[]{:S(2)}) collective-permute-start(f32[3,1024,1]{1,2,0:T(1,128)S(1)} %get-tuple-element.95), channel_id=1, source_target_pairs={{0,1},{1,2},{2,3},{3,4},{4,5},{5,6},{6,7},{7,0},{8,9},{9,10},{10,1... | collective-permute-start | bytes 36872 | tf_op jit(solution)/shard_map/ppermute | solution.py:17
  66.7 2.2 %collective-permute-start.2 = (f32[3,1024,1]{1,2,0:T(1,128)S(1)}, f32[3,1024,1]{1,2,0:T(1,128)S(1)}, u32[]{:S(2)}, u32[]{:S(2)}) collective-permute-start(f32[3,1024,1]{1,2,0:T(1,128)S(1)} %get-tuple-element.90), channel_id=1, source_target_pairs={{1,0},{2,1},{3,2},{4,3},{5,4},{6,5},{7,6},{0,7},{9,8},{10,9},{11,1... | collective-permute-start | bytes 36872 | tf_op jit(solution)/shard_map/ppermute | solution.py:20
  67.5 5.6 %collective-permute-start.3 = (f32[3,1024,1]{1,2,0:T(1,128)S(1)}, f32[3,1024,1]{1,2,0:T(1,128)S(1)}, u32[]{:S(2)}, u32[]{:S(2)}) collective-permute-start(f32[3,1024,1]{1,2,0:T(1,128)S(1)} %get-tuple-element.91), channel_id=1, source_target_pairs={{0,1},{1,2},{2,3},{3,4},{4,5},{5,6},{6,7},{7,0},{8,9},{9,10},{10,1... | collective-permute-start | bytes 36872 | tf_op jit(solution)/shard_map/ppermute | solution.py:17
  74.3 3.2 %collective-permute-start.4 = (f32[3,1024,1]{1,2,0:T(1,128)S(1)}, f32[3,1024,1]{1,2,0:T(1,128)S(1)}, u32[]{:S(2)}, u32[]{:S(2)}) collective-permute-start(f32[3,1024,1]{1,2,0:T(1,128)S(1)} %get-tuple-element.85), channel_id=1, source_target_pairs={{1,0},{2,1},{3,2},{4,3},{5,4},{6,5},{7,6},{0,7},{9,8},{10,9},{11,1... | collective-permute-start | bytes 36872 | tf_op jit(solution)/shard_map/ppermute | solution.py:20
  74.3 5.0 %collective-permute-start.5 = (f32[3,1024,1]{1,2,0:T(1,128)S(1)}, f32[3,1024,1]{1,2,0:T(1,128)S(1)}, u32[]{:S(2)}, u32[]{:S(2)}) collective-permute-start(f32[3,1024,1]{1,2,0:T(1,128)S(1)} %get-tuple-element.84), channel_id=1, source_target_pairs={{0,1},{1,2},{2,3},{3,4},{4,5},{5,6},{6,7},{7,0},{8,9},{9,10},{10,1... | collective-permute-start | bytes 36872 | tf_op jit(solution)/shard_map/ppermute | solution.py:17
  80.8 23.1 %copy-start.7 = (f32[4096]{0:T(1024)S(1)}, f32[4096]{0:T(1024)}, u32[]{:S(2)}) copy-start(f32[4096]{0:T(1024)} %param.21) | copy-start | bytes 49156
  126.5 2.7 %collective-permute-start.6 = (f32[3,1024,1]{1,2,0:T(1,128)S(1)}, f32[3,1024,1]{1,2,0:T(1,128)S(1)}, u32[]{:S(2)}, u32[]{:S(2)}) collective-permute-start(f32[3,1024,1]{1,2,0:T(1,128)S(1)} %get-tuple-element.97), channel_id=1, source_target_pairs={{1,0},{2,1},{3,2},{4,3},{5,4},{6,5},{7,6},{0,7},{9,8},{10,9},{11,1... | collective-permute-start | bytes 36872 | tf_op jit(solution)/shard_map/ppermute | solution.py:20
  127.8 3.7 %collective-permute-start.7 = (f32[3,1024,1]{1,2,0:T(1,128)S(1)}, f32[3,1024,1]{1,2,0:T(1,128)S(1)}, u32[]{:S(2)}, u32[]{:S(2)}) collective-permute-start(f32[3,1024,1]{1,2,0:T(1,128)S(1)} %get-tuple-element.98), channel_id=1, source_target_pairs={{0,1},{1,2},{2,3},{3,4},{4,5},{5,6},{6,7},{7,0},{8,9},{9,10},{10,1... | collective-permute-start | bytes 36872 | tf_op jit(solution)/shard_map/ppermute | solution.py:17
  132.4 2.0 %collective-permute-start.8 = (f32[3,1024,1]{1,2,0:T(1,128)S(1)}, f32[3,1024,1]{1,2,0:T(1,128)S(1)}, u32[]{:S(2)}, u32[]{:S(2)}) collective-permute-start(f32[3,1024,1]{1,2,0:T(1,128)S(1)} %get-tuple-element.77), channel_id=1, source_target_pairs={{1,0},{2,1},{3,2},{4,3},{5,4},{6,5},{7,6},{0,7},{9,8},{10,9},{11,1... | collective-permute-start | bytes 36872 | tf_op jit(solution)/shard_map/ppermute | solution.py:20
  133.0 5.6 %collective-permute-start.9 = (f32[3,1024,1]{1,2,0:T(1,128)S(1)}, f32[3,1024,1]{1,2,0:T(1,128)S(1)}, u32[]{:S(2)}, u32[]{:S(2)}) collective-permute-start(f32[3,1024,1]{1,2,0:T(1,128)S(1)} %get-tuple-element.78), channel_id=1, source_target_pairs={{0,1},{1,2},{2,3},{3,4},{4,5},{5,6},{6,7},{7,0},{8,9},{9,10},{10,1... | collective-permute-start | bytes 36872 | tf_op jit(solution)/shard_map/ppermute | solution.py:17
  139.5 1.5 collective-permute-start.10
  139.6 6.2 %copy-start = (f32[1024,1024]{1,0:T(8,128)S(1)}, f32[1024,1024]{1,0:T(8,128)}, u32[]{:S(2)}) copy-start(f32[1024,1024]{1,0:T(8,128)} %param.18) | copy-start | bytes 12582916
  139.6 6.2 %copy-start.1 = (f32[2,1024,64]{1,2,0:T(8,128)S(1)}, f32[2,1024,64]{1,2,0:T(8,128)}, u32[]{:S(2)}) copy-start(f32[2,1024,64]{1,2,0:T(8,128)} %param.16) | copy-start | bytes 1572868
  139.6 6.2 %copy-start.3 = (f32[2,1024,64]{1,2,0:T(8,128)S(1)}, f32[2,1024,64]{1,2,0:T(8,128)}, u32[]{:S(2)}) copy-start(f32[2,1024,64]{1,2,0:T(8,128)} %param.15) | copy-start | bytes 1572868
  139.6 5.1 %collective-permute-start.11 = (f32[3,1024,1]{1,2,0:T(1,128)S(1)}, f32[3,1024,1]{1,2,0:T(1,128)S(1)}, u32[]{:S(2)}, u32[]{:S(2)}) collective-permute-start(f32[3,1024,1]{1,2,0:T(1,128)S(1)} %get-tuple-element.74), channel_id=1, source_target_pairs={{0,1},{1,2},{2,3},{3,4},{4,5},{5,6},{6,7},{7,0},{8,9},{9,10},{10,1... | collective-permute-start | bytes 36872 | tf_op jit(solution)/shard_map/ppermute | solution.py:17
  145.6 49.8 %copy-start.4 = (f32[2,1024,64]{1,2,0:T(8,128)S(1)}, f32[2,1024,64]{1,2,0:T(8,128)}, u32[]{:S(2)}) copy-start(f32[2,1024,64]{1,2,0:T(8,128)} %param.14) | copy-start | bytes 1572868
Sparse Core Ops, SparseCore 0:
  15.3 44.9 all-gather.2
